TPU v7x, 32 devices: a whole 2x2x4 slice. The times are simulated.
32 devices in a mesh: head: 4 (over y, x), seq: 8 (over z, core).
Axes of the slice: x: 2, y: 2, z: 4, core: 2. Of those that a mesh axis runs over, the one named last changes fastest.
Arguments:
- queries: bfloat16 [4, 8192], P(None, ('head', 'seq')), may hold values from -20 to 20
- key_cache: bfloat16 [4, 8, 8192, 128], P(None, 'head', 'seq'), may hold values from -16 to 16
- value_cache: bfloat16 [4, 8, 8192, 128], P(None, 'head', 'seq'), may hold values from -5 to 5
- page_list: int32 [4, 8, 32], P(None, 'head'), may hold values from 0 to 511, as said below
- shard_counts: int32 [4, 8, 8], P(None, 'head'), may hold values from 0 to 8, as said below
- out_weight: bfloat16 [8192, 8192], P(('head', 'seq')), may hold values from -0.125 to 0.125
Outputs:
- output: bfloat16 [4, 8192], P(None, ('head', 'seq'))
- attention: bfloat16 [4, 8192], P(None, ('head', 'seq'))
- page_mass: float32 [4, 64, 512], P(None, 'head', 'seq')
Inputs may be any that keep to these rules, and one draw needn't show every extreme that they name: With live = the sum of shard_counts[b, g, :], entries 0 to live - 1 of page_list[b, g] are distinct pages in ascending order, and exactly shard_counts[b, g, s] of them lie in pages s * 64 to (s + 1) * 64 - 1; entries from live on are padding. `shard_counts`: exactly 8 for some index s of every batch row and KV head; the sum over s is at most 32.
All inputs are finite; a program needn't handle non-finite values.
Results may differ from a plain program's by a relative error of at most 0.0052.
Values may be sent and summed in bfloat16 or wider, within the bound.
A program may use at most 64 MiB of HBM per device.

v0:
```python
import math

import jax
import jax.numpy as jnp
from jax import lax
from jax.sharding import PartitionSpec as P

HQ = 64
KVH = 8
PAGE = 16
CAP = 8


NEGATIVE = -1e30


def local(queries, key_cache, value_cache, page_list, shard_counts, out_weight):
    batch_rows, kv_local, token_count, head_dim = key_cache.shape
    group_size = HQ // KVH
    pages_local = token_count // PAGE
    shards = lax.axis_size("seq")
    shard_index = lax.axis_index("seq")
    score_scale = 1.0 / math.sqrt(head_dim)
    gathered = lax.all_gather(queries, "seq", axis=1, tiled=True)
    query_heads = gathered.reshape(batch_rows, kv_local, group_size, head_dim)
    page_keys = key_cache.reshape(batch_rows, kv_local, pages_local, PAGE, head_dim)
    lower_keys = jnp.min(page_keys, axis=3).astype(jnp.float32)
    upper_keys = jnp.max(page_keys, axis=3).astype(jnp.float32)
    widened = query_heads.astype(jnp.float32)
    page_bound = (
        jnp.einsum(
            "bgjd,bgpd->bgjp",
            jnp.maximum(widened, 0.0),
            upper_keys,
            precision=lax.Precision.HIGHEST,
        )
        + jnp.einsum(
            "bgjd,bgpd->bgjp",
            jnp.minimum(widened, 0.0),
            lower_keys,
            precision=lax.Precision.HIGHEST,
        )
    ) * score_scale
    page_peak = jnp.max(page_bound, axis=3)
    shard_order = jnp.arange(shards, dtype=jnp.int32)
    offset = jnp.sum(shard_counts * (shard_order < shard_index).astype(jnp.int32), axis=2)
    own_count = jnp.sum(shard_counts * (shard_order == shard_index).astype(jnp.int32), axis=2)
    slot_ids = jnp.arange(CAP, dtype=jnp.int32)
    padded = jnp.concatenate([page_list, jnp.zeros((batch_rows, kv_local, CAP), jnp.int32)], axis=2)
    picked = jnp.take_along_axis(padded, offset[:, :, None] + slot_ids, axis=2)
    slot_valid = slot_ids[None, None, :] < own_count[:, :, None]
    local_pages = jnp.where(slot_valid, picked - shard_index * pages_local, 0)
    flat_keys = key_cache.reshape(batch_rows, kv_local, pages_local, PAGE * head_dim)
    flat_values = value_cache.reshape(batch_rows, kv_local, pages_local, PAGE * head_dim)
    chosen_keys = jnp.take_along_axis(flat_keys, local_pages[:, :, :, None], axis=2).reshape(
        batch_rows, kv_local, CAP * PAGE, head_dim
    )
    chosen_values = jnp.take_along_axis(flat_values, local_pages[:, :, :, None], axis=2).reshape(
        batch_rows, kv_local, CAP * PAGE, head_dim
    )
    live_tokens = jnp.repeat(slot_valid, PAGE, axis=2)
    scores = (
        jnp.einsum("bgjd,bgtd->bgjt", query_heads, chosen_keys, preferred_element_type=jnp.float32)
        * score_scale
    )
    masked = jnp.where(live_tokens[:, :, None, :], scores, NEGATIVE)
    local_top = jnp.max(masked, axis=3)
    global_top = lax.pmax(local_top, "seq")
    page_top = lax.pmax(page_peak, "seq")
    page_terms = jnp.exp(page_bound - page_top[..., None])
    page_sum = lax.psum(jnp.sum(page_terms, axis=3), "seq")
    page_mass = (page_terms / page_sum[..., None]).reshape(
        batch_rows, kv_local * group_size, pages_local
    )
    weights = jnp.where(live_tokens[:, :, None, :], jnp.exp(masked - global_top[..., None]), 0.0)
    local_totals = jnp.sum(weights, axis=3)
    unnormed = jnp.einsum(
        "bgjt,bgtd->bgjd",
        weights.astype(jnp.bfloat16),
        chosen_values,
        preferred_element_type=jnp.float32,
    )
    head_totals = lax.psum(local_totals.reshape(batch_rows, kv_local * group_size), "seq")
    columns = lax.psum_scatter(
        unnormed.reshape(batch_rows, kv_local * group_size * head_dim),
        "seq",
        scatter_dimension=1,
        tiled=True,
    )
    column_width = columns.shape[1]
    column_heads = (
        shard_index * column_width + jnp.arange(column_width, dtype=jnp.int32)
    ) // head_dim
    selector = (
        column_heads[:, None] == jnp.arange(kv_local * group_size, dtype=jnp.int32)[None, :]
    ).astype(jnp.float32)
    column_total = jnp.dot(head_totals, selector.T, precision=lax.Precision.HIGHEST)
    attention = (columns / column_total).astype(jnp.bfloat16)
    out_terms = jnp.dot(attention, out_weight, preferred_element_type=jnp.float32)
    halfway = lax.psum_scatter(out_terms, "head", scatter_dimension=1, tiled=True)
    summed = lax.psum_scatter(halfway, "seq", scatter_dimension=1, tiled=True)
    return (summed.astype(jnp.bfloat16), attention, page_mass)


def solution(mesh):
    return jax.shard_map(
        local,
        mesh=mesh,
        in_specs=(
            P(None, ("head", "seq")),
            P(None, "head", "seq", None),
            P(None, "head", "seq", None),
            P(None, "head", None),
            P(None, "head", None),
            P(("head", "seq"), None),
        ),
        out_specs=(P(None, ("head", "seq")), P(None, ("head", "seq")), P(None, "head", "seq")),
        check_vma=False,
    )
```

profile of v0, /device:TPU:0, one launch (start us, length us, event | category | flops | bytes accessed | tf_op | source)
XLA Modules:
  0.0 187.4 jit_solution(1362484550223251213)
XLA Ops:
  7.2 3.9 %bitcast_reduce_fusion = (bf16[4,2,64,128]{3,2,1,0:T(8,128)(2,1)S(1)}, bf16[4,2,64,128]{3,2,1,0:T(8,128)(2,1)S(1)}) fusion(bf16[4,2,1024,128]{3,2,1,0:T(8,128)(2,1)} %param.9), kind=kLoop, calls=%fused_computation.4 | loop fusion | flops 1966080 | bytes 2359296 | tf_op jit(solution)/shard_map/reduce_min | solution.py:27
  11.2 2.3 %reshape.118 = bf16[4,2,64,2048]{3,2,1,0:T(8,128)(2,1)} reshape(bf16[4,2,1024,128]{3,2,1,0:T(8,128)(2,1)S(1)} %copy-done) | data formatting | bytes 4194304 | tf_op jit(solution)/shard_map/reshape | solution.py:53
  13.5 0.2 multiply_reduce_fusion.1
  14.1 1.0 gather_fusion
  15.6 14.5 %all_gather.3 = bf16[4,2048]{1,0:T(4,128)(2,1)S(1)} all-gather(bf16[4,256]{1,0:T(4,128)(2,1)S(1)} %copy-done.6), channel_id=1, replica_groups=mesh['head'=4,'seq'=8] {'seq'}, dimensions={1}, use_global_device_ids=true | all-gather | bytes 18432 | tf_op jit(solution)/shard_map/all_gather | solution.py:24
  30.1 2.3 %reshape.121 = bf16[4,2,64,2048]{3,2,1,0:T(8,128)(2,1)} reshape(bf16[4,2,1024,128]{3,2,1,0:T(8,128)(2,1)S(1)} %copy-done.2) | data formatting | bytes 4194304 | tf_op jit(solution)/shard_map/reshape | solution.py:54
  32.4 2.4 %gather_fusion.2 = bf16[64,2048]{1,0:T(8,128)(2,1)S(1)} fusion(bf16[4,2,64,2048]{3,2,1,0:T(8,128)(2,1)} %reshape.121, s32[64]{0:T(128)S(1)} %reshape.146), kind=kCustom, calls=%fused_computation.1.clone | custom fusion | bytes 525056 | tf_op jit(solution)/shard_map/jit(take_along_axis)/gather | solution.py:58
  34.8 1.6 gather_fusion.1
  36.7 0.3 fusion.5
  37.0 0.4 fusion.27
  37.4 0.3 fusion.26
  37.8 15.8 %all-reduce.2 = (f32[4,2,8]{2,1,0:T(2,128)S(1)}, f32[4,2,8]{2,1,0:T(2,128)S(1)}) all-reduce(f32[4,2,8]{2,1,0:T(2,128)S(1)} %get-tuple-element.16, f32[4,2,8]{2,1,0:T(2,128)S(1)} %get-tuple-element.18), channel_id=1, replica_groups=mesh['head'=4,'seq'=8] {'seq'}, use_global_device_ids=true, to_apply=%region_3.5 | all-reduce | flops 128 | bytes 1024 | tf_op jit(solution)/shard_map/pmax | solution.py:68
  53.6 0.2 fusion.9
  53.8 1.4 copy.35
  55.3 0.2 fusion.7
  55.7 13.9 %all-reduce.1 = (f32[4,16]{1,0:T(4,128)S(1)}, f32[4,2,8]{2,1,0:T(2,128)S(1)}) all-reduce(f32[4,16]{1,0:T(4,128)S(1)} %reshape.124, f32[4,2,8]{2,1,0:T(2,128)S(1)} %fusion.6), channel_id=1, replica_groups=mesh['head'=4,'seq'=8] {'seq'}, use_global_device_ids=true, to_apply=%region_6.8 | all-reduce | flops 128 | bytes 1024 | tf_op jit(solution)/shard_map/psum | solution.py:83
  69.7 16.4 %reduce-scatter.10.cloned.1.call-done = f32[256,4]{1,0:T(8,128)} async-done(((f32[2048,4]{1,0:T(8,128)}), f32[256,4]{1,0:T(8,128)}) %reduce-scatter.10.cloned.1.call-update) | async-done | bytes 4112
  86.1 1.0 copy.30
  87.1 0.2 fusion.3
  87.4 5.9 %convolution_bitcast_fusion = f32[8192,4]{1,0:T(8,128)} fusion(bf16[4,256]{1,0:T(4,128)(2,1)S(1)} %fusion.3, bf16[256,8192]{1,0:T(8,128)(2,1)} %param.13), kind=kOutput, calls=%fused_computation.3 | convolution fusion | flops 16777216 | bytes 4327424
  93.3 51.1 %reduce-scatter.12.cloned.1.call-done = f32[2048,4]{1,0:T(8,128)} async-done(((f32[8192,4]{1,0:T(8,128)}), f32[2048,4]{1,0:T(8,128)}) %reduce-scatter.12.cloned.1.call-update) | async-done | bytes 32784
  144.4 0.7 divide_bitcast_fusion
  145.1 34.2 %reduce-scatter.14.cloned.1.call-done = f32[256,4]{1,0:T(8,128)} async-done(((f32[2048,4]{1,0:T(8,128)}), f32[256,4]{1,0:T(8,128)}) %reduce-scatter.14.cloned.1.call-update) | async-done | bytes 4112
  179.3 1.6 copy.34
  (39 shorter events, 1.7 us)
Async XLA Ops:
  7.2 4.0 %copy-start = (bf16[4,2,1024,128]{3,2,1,0:T(8,128)(2,1)S(1)}, bf16[4,2,1024,128]{3,2,1,0:T(8,128)(2,1)}, u32[]{:S(2)}) copy-start(bf16[4,2,1024,128]{3,2,1,0:T(8,128)(2,1)} %param.9) | copy-start | bytes 6291460
  7.2 78.9 %reduce-scatter.10.cloned.1.call-start = ((), (), s32[]{:S(2)}) async-start(), calls=%async_computation.3 | async-start | bytes 1179648
  11.2 2.4 %copy-start.3 = (s32[4,2,8]{2,1,0:T(2,128)S(1)}, s32[4,2,8]{2,1,0:T(2,128)}, u32[]{:S(2)}) copy-start(s32[4,2,8]{2,1,0:T(2,128)} %param.12) | copy-start | bytes 772
  11.2 2.9 %copy-start.4 = (s32[4,2,32]{2,1,0:T(2,128)S(1)}, s32[4,2,32]{2,1,0:T(2,128)}, u32[]{:S(2)}) copy-start(s32[4,2,32]{2,1,0:T(2,128)} %param.11) | copy-start | bytes 3076
  14.1 1.5 copy-start.6
  14.1 15.9 %copy-start.2 = (bf16[4,2,1024,128]{3,2,1,0:T(8,128)(2,1)S(1)}, bf16[4,2,1024,128]{3,2,1,0:T(8,128)(2,1)}, u32[]{:S(2)}) copy-start(bf16[4,2,1024,128]{3,2,1,0:T(8,128)(2,1)} %param.10) | copy-start | bytes 6291460
  32.4 2.4 %copy-start.1 = (bf16[4,2,64,2048]{3,2,1,0:T(8,128)(2,1)S(1)}, bf16[4,2,64,2048]{3,2,1,0:T(8,128)(2,1)}, u32[]{:S(2)}) copy-start(bf16[4,2,64,2048]{3,2,1,0:T(8,128)(2,1)} %reshape.118) | copy-start | bytes 6291460
  55.2 89.2 %reduce-scatter.12.cloned.1.call-start = ((), (), s32[]{:S(2)}) async-start(), calls=%async_computation.4 | async-start | bytes 5242880
  87.3 6.0 %copy-start.5 = (bf16[4,256]{1,0:T(4,128)(2,1)}, bf16[4,256]{1,0:T(4,128)(2,1)S(1)}, u32[]{:S(2)}) copy-start(bf16[4,256]{1,0:T(4,128)(2,1)S(1)} %fusion.3) | copy-start | bytes 6148
  93.3 86.0 %reduce-scatter.14.cloned.1.call-start = ((), (), s32[]{:S(2)}) async-start(), calls=%async_computation.5 | async-start | bytes 1179648
Sparse Core Ops, SparseCore 0:
  55.4 30.7 reduce-scatter.9
  93.4 50.9 reduce-scatter.11
  146.7 32.5 reduce-scatter.13
where the time goes:
time: 188 us; the launch traced here: 187 us
  waiting for transfers between devices  102 us (54%)
  blocking collectives  44.2 us (24%)
  local copies, waits for them, and re-layouts  14.4 us (8%)
  between operations  14 us (7%)
  matrix products  7.37 us (4%)
  other arithmetic  5.59 us (3%)
    unnamed x6, waiting for transfers between devices  102 us
    pmax x1, blocking collectives, local(): global_top = lax.pmax(local_top, 'seq')  15.8 us
    all_gather x1, blocking collectives, local(): gathered = lax.all_gather(queries, 'seq', axis=1, tiled=True)  14.5 us
    psum x1, blocking collectives, local(): lax.psum(local_totals.reshape(batch_rows, kv_local * group_size), 'seq')  13.9 us
    unnamed x1, matrix products  5.89 us
    unnamed x17, local copies, waits for them, and re-layouts  3.98 us
    reduce_min x1, other arithmetic, local(): lower_keys = jnp.min(page_keys, axis=3).astype(jnp.float32)  3.94 us
  transfers between devices with their start and end apart: 3, of which 3 were waited for; matrix products, arithmetic and copies ran while one was open for 1% of the time, Pallas kernels for 0%

commit v1 on v0

--- a/solution.py
+++ b/solution.py
@@ -1,8 +1,11 @@
+import functools
 import math
 
 import jax
 import jax.numpy as jnp
 from jax import lax
+from jax.experimental import pallas as pl
+from jax.experimental.pallas import tpu as pltpu
 from jax.sharding import PartitionSpec as P
 
 HQ = 64
@@ -102,9 +105,317 @@
     return (summed.astype(jnp.bfloat16), attention, page_mass)
 
 
+F32 = jnp.float32
+BF16 = jnp.bfloat16
+MESH = pl.DeviceIdType.MESH
+NT = (((1,), (1,)), ((), ()))
+
+
+def spread(row, first, count, offset):
+    shape = (count, row.shape[1])
+    sub = lax.broadcasted_iota(jnp.int32, shape, 0)
+    lane = lax.broadcasted_iota(jnp.int32, shape, 1)
+    return jnp.sum(jnp.where(lane == sub + (first + offset), row, 0.0), axis=1, keepdims=True)
+
+
+def kernel(
+    H, S,
+    q_ref, list_ref, count_ref, k_hbm, v_hbm, w_hbm,
+    out_ref, attn_ref, mass_ref,
+    kbuf, vbuf, wbuf, qsend, qrecv, qf, hi, lo, kcat, bias, bound_buf,
+    stsend, strecv, usend, urecv, psend, precv,
+    ksem, vsem, wsem, qss, qrs, sss, srs, uss, urs, pss, prs,
+):
+    B, KV, T, HD = k_hbm.shape
+    G = HQ // KVH
+    PG = T // PAGE
+    ROWS = B * KV * G
+    CW = q_ref.shape[1]
+    HO = CW // HD
+    SLOTS = list_ref.shape[2]
+    scale = 1.0 / math.sqrt(HD)
+    h = lax.axis_index("head")
+    s = lax.axis_index("seq")
+    pairs = [(b, g) for b in range(B) for g in range(KV)]
+    far = sorted(range(1, S), key=lambda d: -min(d, S - d))
+
+    def seq_peer(d):
+        return lax.rem(s + d, S)
+
+    def head_peer(d):
+        return lax.rem(h + d, H)
+
+    barrier = pltpu.get_barrier_semaphore()
+    for dh in range(H):
+        for ds in range(S):
+            if dh or ds:
+                pl.semaphore_signal(
+                    barrier, inc=1, device_id=(head_peer(dh), seq_peer(ds)), device_id_type=MESH
+                )
+    kcopies = [
+        pltpu.make_async_copy(k_hbm.at[b, g], kbuf.at[n], ksem.at[n]) for n, (b, g) in enumerate(pairs)
+    ]
+    vcopies = [
+        pltpu.make_async_copy(v_hbm.at[b, g], vbuf.at[n], vsem.at[n]) for n, (b, g) in enumerate(pairs)
+    ]
+    wcopy = pltpu.make_async_copy(w_hbm, wbuf, wsem)
+    for c in kcopies + vcopies:
+        c.start()
+    wcopy.start()
+
+    q = q_ref[...].astype(F32)
+    own_q = jnp.concatenate([q[:, i * HD : (i + 1) * HD] for i in range(HO)], axis=0).astype(BF16)
+    qsend[...] = own_q
+
+    sub = lax.broadcasted_iota(jnp.int32, (len(pairs), HD), 0)
+    lane = lax.broadcasted_iota(jnp.int32, (len(pairs), HD), 1)
+    columns = [jnp.full((len(pairs), HD), -1, jnp.int32) for _ in range(CAP)]
+    for n, (b, g) in enumerate(pairs):
+        offset = jnp.int32(0)
+        for j in range(S):
+            offset = offset + jnp.where(j < s, count_ref[b, g, j], 0)
+        own = count_ref[b, g, s]
+        for c in range(CAP):
+            page = list_ref[b, g, jnp.minimum(offset + c, SLOTS - 1)] - s * PG
+            page = jnp.where(c < own, page, -1)
+            columns[c] = jnp.where(sub == n, page, columns[c])
+    for v in range(T // HD):
+        pid = (lane + v * HD) // PAGE
+        hit = pid == columns[0]
+        for c in range(1, CAP):
+            hit = hit | (pid == columns[c])
+        bias[:, v * HD : (v + 1) * HD] = jnp.where(hit, 0.0, NEGATIVE)
+
+    def bounds_of(n):
+        kcopies[n].wait()
+        x = kbuf[n].astype(F32).reshape(PG, 2, PAGE // 2, HD)
+        hi[...] = jnp.max(x, axis=1).reshape(PG * PAGE // 2, HD)
+        lo[...] = jnp.min(x, axis=1).reshape(PG * PAGE // 2, HD)
+        step = PAGE // 2
+        up = hi[pl.ds(0, PG, stride=step), :]
+        down = lo[pl.ds(0, PG, stride=step), :]
+        for i in range(1, step):
+            up = jnp.maximum(up, hi[pl.ds(i, PG, stride=step), :])
+            down = jnp.minimum(down, lo[pl.ds(i, PG, stride=step), :])
+        kcat[n] = jnp.concatenate([up, down], axis=1).astype(BF16)
+
+    half = len(pairs) // 2
+    for n in range(half):
+        bounds_of(n)
+
+    pl.semaphore_wait(barrier, H * S - 1)
+
+    def seq_copies(src_of, dst, send, recv):
+        copies = []
+        for ds in far:
+            t = seq_peer(ds)
+            copies.append(
+                pltpu.make_async_remote_copy(
+                    src_ref=src_of(t),
+                    dst_ref=dst.at[s],
+                    send_sem=send.at[ds],
+                    recv_sem=recv.at[s],
+                    device_id=(h, t),
+                    device_id_type=MESH,
+                )
+            )
+        for c in copies:
+            c.start()
+        return copies
+
+    def seq_wait(src_of, dst, send, recv):
+        for ds in range(1, S):
+            t = seq_peer(ds)
+            pltpu.make_async_remote_copy(
+                src_ref=src_of(t),
+                dst_ref=dst.at[t],
+                send_sem=send.at[ds],
+                recv_sem=recv.at[t],
+                device_id=(h, t),
+                device_id_type=MESH,
+            ).wait_recv()
+
+    sent = []
+    q_src = lambda t: qsend
+    sent += seq_copies(q_src, qrecv, qss, qrs)
+    qrecv[s] = own_q
+    for n in range(half, len(pairs)):
+        bounds_of(n)
+    seq_wait(q_src, qrecv, qss, qrs)
+
+    qf[...] = qrecv[...].astype(F32).reshape(ROWS, HD)
+    lane8 = lax.broadcasted_iota(jnp.int32, (G, HD), 1)
+    sub8 = lax.broadcasted_iota(jnp.int32, (G, HD), 0)
+    scores, bounds = [], []
+    for n, (b, g) in enumerate(pairs):
+        heads = qf[pl.ds(g * G * B + b, G, stride=B), :]
+        scores.append(
+            lax.dot_general(heads.astype(BF16), kbuf[n], NT, preferred_element_type=F32) * scale
+            + bias[n : n + 1, :]
+        )
+        signed = jnp.concatenate([jnp.maximum(heads, 0.0), jnp.minimum(heads, 0.0)], axis=1)
+        bounds.append(lax.dot_general(signed.astype(BF16), kcat[n], NT, preferred_element_type=F32) * scale)
+    tops = [jnp.max(x, axis=1, keepdims=True) for x in scores]
+    peaks = [jnp.max(x, axis=1, keepdims=True) for x in bounds]
+    weights = [jnp.exp(x - m) for x, m in zip(scores, tops)]
+    totals = [jnp.sum(x, axis=1, keepdims=True) for x in weights]
+    sums = [jnp.sum(jnp.exp(x - m), axis=1, keepdims=True) for x, m in zip(bounds, peaks)]
+    soft = jnp.zeros((G, HD), F32)
+    page = jnp.zeros((G, HD), F32)
+    for n in range(len(pairs)):
+        first = lane8 == sub8 + n * G
+        second = lane8 == sub8 + (n * G + ROWS)
+        soft = jnp.where(first, tops[n], jnp.where(second, totals[n], soft))
+        page = jnp.where(first, peaks[n], jnp.where(second, sums[n], page))
+        bound_buf[n] = bounds[n]
+    stats = jnp.concatenate(
+        [jnp.sum(soft, axis=0, keepdims=True), jnp.sum(page, axis=0, keepdims=True)], axis=0
+    )
+    stsend[...] = stats
+    st_src = lambda t: stsend
+    sent += seq_copies(st_src, strecv, sss, srs)
+    strecv[s] = stats
+
+    for c in vcopies:
+        c.wait()
+    for n, (b, g) in enumerate(pairs):
+        usend[pl.ds(g * G * B + b, G, stride=B), :] = jnp.dot(
+            weights[n].astype(BF16), vbuf[n], preferred_element_type=F32
+        )
+    R = HO * B
+    u_src = lambda t: usend.at[pl.ds(pl.multiple_of(t * R, R), R), :]
+    sent += seq_copies(u_src, urecv, uss, urs)
+    urecv[s] = usend[pl.ds(pl.multiple_of(s * R, R), R), :]
+
+    seq_wait(st_src, strecv, sss, srs)
+    soft_all = strecv[:, 0, :]
+    page_all = strecv[:, 1, :]
+    soft_scale = jnp.exp(soft_all - jnp.max(soft_all, axis=0, keepdims=True))
+    soft_total = jnp.sum(pltpu.roll(soft_all, ROWS, 1) * soft_scale, axis=0, keepdims=True)
+    subr = lax.broadcasted_iota(jnp.int32, (R, HD), 0)
+    laner = lax.broadcasted_iota(jnp.int32, (R, HD), 1)
+    mine = laner == (subr % B) * (KV * G) + s * HO + subr // B
+
+    def column(row):
+        return jnp.sum(jnp.where(mine, row, 0.0), axis=1, keepdims=True)
+
+    factors = [column(soft_scale[p : p + 1]) for p in range(S)]
+    total = column(soft_total)
+
+    wcopy.wait()
+    seq_wait(u_src, urecv, uss, urs)
+    unnormed = factors[0] * urecv[0]
+    for p in range(1, S):
+        unnormed = unnormed + factors[p] * urecv[p]
+    normed = unnormed / total
+    attention = jnp.concatenate([normed[i * B : (i + 1) * B] for i in range(HO)], axis=1).astype(BF16)
+    attn_ref[...] = attention
+
+    def out_copy(dh, ts, slot):
+        return pltpu.make_async_remote_copy(
+            src_ref=psend.at[dh * S + ts],
+            dst_ref=precv.at[slot],
+            send_sem=pss.at[dh * S + ts],
+            recv_sem=prs.at[slot],
+            device_id=(head_peer(dh), ts),
+            device_id_type=MESH,
+        )
+
+    for dh in list(range(1, H)) + [0]:
+        start = pl.multiple_of(head_peer(dh) * (S * CW), S * CW)
+        terms = jnp.dot(attention, wbuf[:, pl.ds(start, S * CW)], preferred_element_type=F32)
+        for j in range(S):
+            for i in range(HO):
+                psend[dh * S + j, i * B : (i + 1) * B, :] = terms[:, j * CW + i * HD : j * CW + (i + 1) * HD]
+        for ds in far + [0]:
+            if dh or ds:
+                c = out_copy(dh, seq_peer(ds), dh * S + s)
+                c.start()
+                sent.append(c)
+    precv[s] = psend[s]
+
+    page_peak = jnp.max(page_all, axis=0, keepdims=True)
+    page_sum = jnp.sum(
+        pltpu.roll(page_all, ROWS, 1) * jnp.exp(page_all - page_peak), axis=0, keepdims=True
+    )
+    for n, (b, g) in enumerate(pairs):
+        peak = spread(page_peak, n * G, G, 0)
+        mass = spread(page_sum, n * G, G, 0)
+        mass_ref[b, g * G : (g + 1) * G, :] = jnp.exp(bound_buf[n] - peak) / mass
+
+    for dh in range(H):
+        for ds in range(S):
+            if dh or ds:
+                slot = dh * S + seq_peer(ds)
+                out_copy(dh, seq_peer(ds), slot).wait_recv()
+    summed = precv[0]
+    for slot in range(1, H * S):
+        summed = summed + precv[slot]
+    out_ref[...] = jnp.concatenate([summed[i * B : (i + 1) * B] for i in range(HO)], axis=1).astype(BF16)
+    for c in sent:
+        c.wait_send()
+
+
+def fused(queries, key_cache, value_cache, page_list, shard_counts, out_weight):
+    B, KV, T, HD = key_cache.shape
+    H, S = lax.axis_size("head"), lax.axis_size("seq")
+    G = HQ // KVH
+    CW = queries.shape[1]
+    R = CW // HD * B
+    N, PG, ROWS = B * KV, T // PAGE, B * KV * G
+    vmem = pl.BlockSpec(memory_space=pltpu.VMEM)
+    smem = pl.BlockSpec(memory_space=pltpu.SMEM)
+    hbm = pl.BlockSpec(memory_space=pl.ANY)
+    dma = pltpu.SemaphoreType.DMA
+    return pl.pallas_call(
+        functools.partial(kernel, H, S),
+        out_shape=(
+            jax.ShapeDtypeStruct((B, CW), BF16),
+            jax.ShapeDtypeStruct((B, CW), BF16),
+            jax.ShapeDtypeStruct((B, KV * G, PG), F32),
+        ),
+        in_specs=[vmem, smem, smem, hbm, hbm, hbm],
+        out_specs=(vmem, vmem, vmem),
+        scratch_shapes=[
+            pltpu.VMEM((N, T, HD), BF16),
+            pltpu.VMEM((N, T, HD), BF16),
+            pltpu.VMEM(out_weight.shape, BF16),
+            pltpu.VMEM((R, HD), BF16),
+            pltpu.VMEM((S, R, HD), BF16),
+            pltpu.VMEM((ROWS, HD), F32),
+            pltpu.VMEM((T // 2, HD), F32),
+            pltpu.VMEM((T // 2, HD), F32),
+            pltpu.VMEM((N, PG, 2 * HD), BF16),
+            pltpu.VMEM((N, T), F32),
+            pltpu.VMEM((N, G, PG), F32),
+            pltpu.VMEM((2, HD), F32),
+            pltpu.VMEM((S, 2, HD), F32),
+            pltpu.VMEM((ROWS, HD), F32),
+            pltpu.VMEM((S, R, HD), F32),
+            pltpu.VMEM((H * S, R, HD), F32),
+            pltpu.VMEM((H * S, R, HD), F32),
+            dma((N,)), dma((N,)), dma,
+            dma((S,)), dma((S,)), dma((S,)), dma((S,)), dma((S,)), dma((S,)),
+            dma((H * S,)), dma((H * S,)),
+        ],
+        compiler_params=pltpu.CompilerParams(
+            collective_id=0, has_side_effects=True, vmem_limit_bytes=56 * 1024 * 1024
+        ),
+    )(queries, page_list, shard_counts, key_cache, value_cache, out_weight)
+
+
+def whole_heads(queries, key_cache, value_cache, page_list, shard_counts, out_weight):
+    B, KV, T, HD = key_cache.shape
+    CW = queries.shape[1]
+    rows = B * KV * (HQ // KVH)
+    fits = CW % HD == 0 and (CW // HD * B) % 8 == 0 and B * KV == 8 and 2 * rows <= HD
+    run = fused if fits else local
+    return run(queries, key_cache, value_cache, page_list, shard_counts, out_weight)
+
+
 def solution(mesh):
     return jax.shard_map(
-        local,
+        whole_heads,
         mesh=mesh,
         in_specs=(
             P(None, ("head", "seq")),

time: 188 us -> 27.8 us (0.15)
  waiting for transfers between devices: 102 us -> 0 us
  blocking collectives: 44.2 us -> 0 us
  Pallas kernels: 0 us -> 23 us
  between operations: 14 us -> 0.64 us
  local copies, waits for them, and re-layouts: 14.4 us -> 3.86 us
  matrix products: 7.37 us -> 0 us
  other arithmetic: 5.59 us -> 0 us
    unnamed x6 -> x0, waiting for transfers between devices: 102 us -> none
    pallas_call x0 -> x1, Pallas kernels: none -> 23 us  [fused(): pl.pallas_call(functools.partial(kernel, H, S), out_shape=(jax.ShapeDtype...]
    pmax x1 -> x0, blocking collectives: 15.8 us -> none  [local(): global_top = lax.pmax(local_top, 'seq')]
    all_gather x1 -> x0, blocking collectives: 14.5 us -> none  [local(): gathered = lax.all_gather(queries, 'seq', axis=1, tiled=True)]
    psum x1 -> x0, blocking collectives: 13.9 us -> none  [local(): lax.psum(local_totals.reshape(batch_rows, kv_local * group_size), 'seq')]
    unnamed x1 -> x0, matrix products: 5.89 us -> none
    gather x6 -> x0, local copies, waits for them, and re-layouts: 5.18 us -> none  [the longest x1 2.41 us: local(): jnp.take_along_axis(flat_values, local_pages[:, :, :, None], axis=2)]
    reshape x5 -> x0, local copies, waits for them, and re-layouts: 4.97 us -> none  [the longest x1 2.33 us: local(): key_cache.reshape(batch_rows, kv_local, pages_local, PAGE * head_dim)]
  transfers between devices with their start and end apart: 3 -> 0, of which waited for: 3 -> 0; matrix products, arithmetic and copies ran while one was open for 1% -> 0% of each run, Pallas kernels for 0% -> 0%
where the time goes in v1:
time: 27.8 us; the launch traced here: 27.5 us
  Pallas kernels  23 us (83%)
  local copies, waits for them, and re-layouts  3.86 us (14%)
  between operations  0.64 us (2%)
    pallas_call x1, Pallas kernels, fused(): pl.pallas_call(functools.partial(kernel, H, S), out_shape=(jax.ShapeDtype...  23 us
    unnamed x3, local copies, waits for them, and re-layouts  3.86 us

profile of v1, /device:TPU:0, one launch (start us, length us, event | category | flops | bytes accessed | tf_op | source)
XLA Modules:
  0.0 27.5 jit_solution(3188418018343089)
XLA Ops:
  0.6 23.0 %shard_map.85 = (bf16[4,256]{1,0:T(4,128)(2,1)}, bf16[4,256]{1,0:T(4,128)(2,1)}, f32[4,16,64]{2,1,0:T(8,128)}) custom-call(bf16[4,256]{1,0:T(4,128)(2,1)} %q_ref.1, s32[4,2,32]{2,1,0:T(2,128)} %list_ref.1, s32[4,2,8]{2,1,0:T(2,128)} %count_ref.1, bf16[4,2,1024,128]{3,2,1,0:T(8,128)(2,1)} %k_hbm.1, bf16[4,2,1024,128]{3,2,1,0:T(8,128)(2,1)} %v_hbm.1, ...), custom_call_target="tpu_custom_call" | custom-call | tf_op jit(solution)/shard_map/pallas_call | solution.py:370
  23.6 1.2 %copy.12 = bf16[4,256]{1,0:T(4,128)(2,1)} copy(bf16[4,256]{1,0:T(4,128)(2,1)} %get-tuple-element.6) | data formatting | bytes 4096
  24.9 1.2 %copy.13 = bf16[4,256]{1,0:T(4,128)(2,1)} copy(bf16[4,256]{1,0:T(4,128)(2,1)} %get-tuple-element.7) | data formatting | bytes 4096
  26.1 1.4 %copy.14 = f32[4,16,64]{2,1,0:T(8,128)} copy(f32[4,16,64]{2,1,0:T(8,128)} %get-tuple-element.8) | data formatting | bytes 32768

commit v2 on v1

--- a/solution.py
+++ b/solution.py
@@ -107,6 +107,9 @@
 
 F32 = jnp.float32
 BF16 = jnp.bfloat16
+SENT = jnp.float32
+EARLY = 4
+TURN = True
 MESH = pl.DeviceIdType.MESH
 NT = (((1,), (1,)), ((), ()))
 
@@ -120,11 +123,11 @@
 
 def kernel(
     H, S,
-    q_ref, list_ref, count_ref, k_hbm, v_hbm, w_hbm,
-    out_ref, attn_ref, mass_ref,
-    kbuf, vbuf, wbuf, qsend, qrecv, qf, hi, lo, kcat, bias, bound_buf,
-    stsend, strecv, usend, urecv, psend, precv,
-    ksem, vsem, wsem, qss, qrs, sss, srs, uss, urs, pss, prs,
+    q_hbm, list_hbm, count_hbm, k_hbm, v_hbm, w_hbm,
+    sum_ref, attn_ref, mass_ref,
+    q_ref, list_ref, count_ref, kbuf, kturn, vbuf, wbuf, qsend, qrecv, qf, hi, lo, kcat, bias, bound_buf,
+    stsend, strecv, pgsend, pgrecv, usend, urecv, psend, precv,
+    isem, ksem, vsem, wsem, qss, qrs, sss, srs, uss, urs, gss, grs, pss, prs,
 ):
     B, KV, T, HD = k_hbm.shape
     G = HQ // KVH
@@ -152,6 +155,13 @@
                 pl.semaphore_signal(
                     barrier, inc=1, device_id=(head_peer(dh), seq_peer(ds)), device_id_type=MESH
                 )
+    icopies = [
+        pltpu.make_async_copy(q_hbm, q_ref, isem.at[0]),
+        pltpu.make_async_copy(list_hbm, list_ref, isem.at[1]),
+        pltpu.make_async_copy(count_hbm, count_ref, isem.at[2]),
+    ]
+    for c in icopies:
+        c.start()
     kcopies = [
         pltpu.make_async_copy(k_hbm.at[b, g], kbuf.at[n], ksem.at[n]) for n, (b, g) in enumerate(pairs)
     ]
@@ -163,6 +173,8 @@
         c.start()
     wcopy.start()
 
+    for c in icopies:
+        c.wait()
     q = q_ref[...].astype(F32)
     own_q = jnp.concatenate([q[:, i * HD : (i + 1) * HD] for i in range(HO)], axis=0).astype(BF16)
     qsend[...] = own_q
@@ -188,6 +200,8 @@
 
     def bounds_of(n):
         kcopies[n].wait()
+        if TURN:
+            kturn[n] = kbuf[n].T
         x = kbuf[n].astype(F32).reshape(PG, 2, PAGE // 2, HD)
         hi[...] = jnp.max(x, axis=1).reshape(PG * PAGE // 2, HD)
         lo[...] = jnp.min(x, axis=1).reshape(PG * PAGE // 2, HD)
@@ -199,7 +213,12 @@
             down = jnp.minimum(down, lo[pl.ds(i, PG, stride=step), :])
         kcat[n] = jnp.concatenate([up, down], axis=1).astype(BF16)
 
-    half = len(pairs) // 2
+    def score_of(n, heads):
+        if TURN:
+            return jnp.dot(heads, kturn[n], preferred_element_type=F32)
+        return lax.dot_general(heads, kbuf[n], NT, preferred_element_type=F32)
+
+    half = EARLY
     for n in range(half):
         bounds_of(n)
 
@@ -246,31 +265,22 @@
     qf[...] = qrecv[...].astype(F32).reshape(ROWS, HD)
     lane8 = lax.broadcasted_iota(jnp.int32, (G, HD), 1)
     sub8 = lax.broadcasted_iota(jnp.int32, (G, HD), 0)
-    scores, bounds = [], []
-    for n, (b, g) in enumerate(pairs):
-        heads = qf[pl.ds(g * G * B + b, G, stride=B), :]
-        scores.append(
-            lax.dot_general(heads.astype(BF16), kbuf[n], NT, preferred_element_type=F32) * scale
-            + bias[n : n + 1, :]
-        )
-        signed = jnp.concatenate([jnp.maximum(heads, 0.0), jnp.minimum(heads, 0.0)], axis=1)
-        bounds.append(lax.dot_general(signed.astype(BF16), kcat[n], NT, preferred_element_type=F32) * scale)
+    queries = [qf[pl.ds(g * G * B + b, G, stride=B), :] for b, g in pairs]
+    scores = [
+        score_of(n, queries[n].astype(BF16)) * scale + bias[n : n + 1, :] for n in range(len(pairs))
+    ]
     tops = [jnp.max(x, axis=1, keepdims=True) for x in scores]
-    peaks = [jnp.max(x, axis=1, keepdims=True) for x in bounds]
     weights = [jnp.exp(x - m) for x, m in zip(scores, tops)]
     totals = [jnp.sum(x, axis=1, keepdims=True) for x in weights]
-    sums = [jnp.sum(jnp.exp(x - m), axis=1, keepdims=True) for x, m in zip(bounds, peaks)]
-    soft = jnp.zeros((G, HD), F32)
-    page = jnp.zeros((G, HD), F32)
-    for n in range(len(pairs)):
-        first = lane8 == sub8 + n * G
-        second = lane8 == sub8 + (n * G + ROWS)
-        soft = jnp.where(first, tops[n], jnp.where(second, totals[n], soft))
-        page = jnp.where(first, peaks[n], jnp.where(second, sums[n], page))
-        bound_buf[n] = bounds[n]
-    stats = jnp.concatenate(
-        [jnp.sum(soft, axis=0, keepdims=True), jnp.sum(page, axis=0, keepdims=True)], axis=0
-    )
+
+    def packed(left, right):
+        tile = jnp.zeros((G, HD), F32)
+        for n in range(len(pairs)):
+            tile = jnp.where(lane8 == sub8 + n * G, left[n], tile)
+            tile = jnp.where(lane8 == sub8 + (n * G + ROWS), right[n], tile)
+        return jnp.sum(tile, axis=0, keepdims=True)
+
+    stats = packed(tops, totals)
     stsend[...] = stats
     st_src = lambda t: stsend
     sent += seq_copies(st_src, strecv, sss, srs)
@@ -287,9 +297,21 @@
     sent += seq_copies(u_src, urecv, uss, urs)
     urecv[s] = usend[pl.ds(pl.multiple_of(s * R, R), R), :]
 
+    bounds = []
+    for n in range(len(pairs)):
+        signed = jnp.concatenate([jnp.maximum(queries[n], 0.0), jnp.minimum(queries[n], 0.0)], axis=1)
+        bounds.append(lax.dot_general(signed.astype(BF16), kcat[n], NT, preferred_element_type=F32) * scale)
+        bound_buf[n] = bounds[n]
+    peaks = [jnp.max(x, axis=1, keepdims=True) for x in bounds]
+    sums = [jnp.sum(jnp.exp(x - m), axis=1, keepdims=True) for x, m in zip(bounds, peaks)]
+    page_stats = packed(peaks, sums)
+    pgsend[...] = page_stats
+    pg_src = lambda t: pgsend
+    sent += seq_copies(pg_src, pgrecv, gss, grs)
+    pgrecv[s] = page_stats
+
     seq_wait(st_src, strecv, sss, srs)
     soft_all = strecv[:, 0, :]
-    page_all = strecv[:, 1, :]
     soft_scale = jnp.exp(soft_all - jnp.max(soft_all, axis=0, keepdims=True))
     soft_total = jnp.sum(pltpu.roll(soft_all, ROWS, 1) * soft_scale, axis=0, keepdims=True)
     subr = lax.broadcasted_iota(jnp.int32, (R, HD), 0)
@@ -310,6 +332,9 @@
     normed = unnormed / total
     attention = jnp.concatenate([normed[i * B : (i + 1) * B] for i in range(HO)], axis=1).astype(BF16)
     attn_ref[...] = attention
+
+    def stacked(x):
+        return jnp.concatenate([x[:, i * HD : (i + 1) * HD] for i in range(HO)], axis=0)
 
     def out_copy(dh, ts, slot):
         return pltpu.make_async_remote_copy(
@@ -325,8 +350,7 @@
         start = pl.multiple_of(head_peer(dh) * (S * CW), S * CW)
         terms = jnp.dot(attention, wbuf[:, pl.ds(start, S * CW)], preferred_element_type=F32)
         for j in range(S):
-            for i in range(HO):
-                psend[dh * S + j, i * B : (i + 1) * B, :] = terms[:, j * CW + i * HD : j * CW + (i + 1) * HD]
+            psend[dh * S + j] = stacked(terms[:, j * CW : (j + 1) * CW]).astype(SENT)
         for ds in far + [0]:
             if dh or ds:
                 c = out_copy(dh, seq_peer(ds), dh * S + s)
@@ -334,6 +358,8 @@
                 sent.append(c)
     precv[s] = psend[s]
 
+    seq_wait(pg_src, pgrecv, gss, grs)
+    page_all = pgrecv[:, 0, :]
     page_peak = jnp.max(page_all, axis=0, keepdims=True)
     page_sum = jnp.sum(
         pltpu.roll(page_all, ROWS, 1) * jnp.exp(page_all - page_peak), axis=0, keepdims=True
@@ -348,12 +374,21 @@
             if dh or ds:
                 slot = dh * S + seq_peer(ds)
                 out_copy(dh, seq_peer(ds), slot).wait_recv()
-    summed = precv[0]
+    summed = precv[0].astype(F32)
     for slot in range(1, H * S):
-        summed = summed + precv[slot]
-    out_ref[...] = jnp.concatenate([summed[i * B : (i + 1) * B] for i in range(HO)], axis=1).astype(BF16)
+        summed = summed + precv[slot].astype(F32)
+    sum_ref[...] = summed
     for c in sent:
         c.wait_send()
+
+
+def finish(sum_ref, attn_in, mass_in, out_ref, attn_ref, mass_ref):
+    B, CW = out_ref.shape
+    HD = sum_ref.shape[1]
+    rows = sum_ref[...]
+    out_ref[...] = jnp.concatenate([rows[i * B : (i + 1) * B] for i in range(CW // HD)], axis=1).astype(BF16)
+    attn_ref[...] = attn_in[...]
+    mass_ref[...] = mass_in[...]
 
 
 def fused(queries, key_cache, value_cache, page_list, shard_counts, out_weight):
@@ -364,20 +399,23 @@
     R = CW // HD * B
     N, PG, ROWS = B * KV, T // PAGE, B * KV * G
     vmem = pl.BlockSpec(memory_space=pltpu.VMEM)
-    smem = pl.BlockSpec(memory_space=pltpu.SMEM)
     hbm = pl.BlockSpec(memory_space=pl.ANY)
     dma = pltpu.SemaphoreType.DMA
-    return pl.pallas_call(
+    partial_outs = pl.pallas_call(
         functools.partial(kernel, H, S),
         out_shape=(
-            jax.ShapeDtypeStruct((B, CW), BF16),
-            jax.ShapeDtypeStruct((B, CW), BF16),
-            jax.ShapeDtypeStruct((B, KV * G, PG), F32),
+            pltpu.VMEM((R, HD), F32),
+            pltpu.VMEM((B, CW), BF16),
+            pltpu.VMEM((B, KV * G, PG), F32),
         ),
-        in_specs=[vmem, smem, smem, hbm, hbm, hbm],
+        in_specs=[hbm] * 6,
         out_specs=(vmem, vmem, vmem),
         scratch_shapes=[
+            pltpu.VMEM((B, CW), BF16),
+            pltpu.SMEM(page_list.shape, jnp.int32),
+            pltpu.SMEM(shard_counts.shape, jnp.int32),
             pltpu.VMEM((N, T, HD), BF16),
+            pltpu.VMEM((N, HD, T), BF16),
             pltpu.VMEM((N, T, HD), BF16),
             pltpu.VMEM(out_weight.shape, BF16),
             pltpu.VMEM((R, HD), BF16),
@@ -388,20 +426,32 @@
             pltpu.VMEM((N, PG, 2 * HD), BF16),
             pltpu.VMEM((N, T), F32),
             pltpu.VMEM((N, G, PG), F32),
-            pltpu.VMEM((2, HD), F32),
-            pltpu.VMEM((S, 2, HD), F32),
+            pltpu.VMEM((1, HD), F32),
+            pltpu.VMEM((S, 1, HD), F32),
+            pltpu.VMEM((1, HD), F32),
+            pltpu.VMEM((S, 1, HD), F32),
             pltpu.VMEM((ROWS, HD), F32),
             pltpu.VMEM((S, R, HD), F32),
-            pltpu.VMEM((H * S, R, HD), F32),
-            pltpu.VMEM((H * S, R, HD), F32),
-            dma((N,)), dma((N,)), dma,
-            dma((S,)), dma((S,)), dma((S,)), dma((S,)), dma((S,)), dma((S,)),
+            pltpu.VMEM((H * S, R, HD), SENT),
+            pltpu.VMEM((H * S, R, HD), SENT),
+            dma((3,)), dma((N,)), dma((N,)), dma,
+            dma((S,)), dma((S,)), dma((S,)), dma((S,)), dma((S,)), dma((S,)), dma((S,)), dma((S,)),
             dma((H * S,)), dma((H * S,)),
         ],
         compiler_params=pltpu.CompilerParams(
             collective_id=0, has_side_effects=True, vmem_limit_bytes=56 * 1024 * 1024
         ),
     )(queries, page_list, shard_counts, key_cache, value_cache, out_weight)
+    return pl.pallas_call(
+        finish,
+        out_shape=(
+            jax.ShapeDtypeStruct((B, CW), BF16),
+            jax.ShapeDtypeStruct((B, CW), BF16),
+            jax.ShapeDtypeStruct((B, KV * G, PG), F32),
+        ),
+        in_specs=[vmem] * 3,
+        out_specs=(vmem, vmem, vmem),
+    )(*(pltpu.with_memory_space_constraint(x, pltpu.VMEM) for x in partial_outs))
 
 
 def whole_heads(queries, key_cache, value_cache, page_list, shard_counts, out_weight):

time: 27.8 us -> 23.3 us (0.84)
  local copies, waits for them, and re-layouts: 3.86 us -> 0 us
  Pallas kernels: 23 us -> 22.5 us
    unnamed x3 -> x0, local copies, waits for them, and re-layouts: 3.86 us -> none
    pallas_call x1 -> x2, Pallas kernels: 23 us -> 22.5 us  [the longest x1 21.8 us: fused(): pl.pallas_call(functools.partial(kernel, H, S), out_shape=(pltpu.VMEM((R,...]
where the time goes in v2:
time: 23.3 us; the launch traced here: 23.1 us
  Pallas kernels  22.5 us (97%)
  between operations  0.64 us (3%)
    pallas_call x1, Pallas kernels, fused(): pl.pallas_call(functools.partial(kernel, H, S), out_shape=(pltpu.VMEM((R,...  21.8 us
    pallas_call x1, Pallas kernels, fused(): pl.pallas_call(finish, out_shape=(jax.ShapeDtypeStruct((B, CW), BF16), ja...  0.63 us

profile of v2, /device:TPU:0, one launch (start us, length us, event | category | flops | bytes accessed | tf_op | source)
XLA Modules:
  0.0 23.1 jit_solution(9389344826313249642)
XLA Ops:
  0.6 21.8 %shard_map.85 = (f32[8,128]{1,0:T(8,128)S(1)}, bf16[4,256]{1,0:T(4,128)(2,1)S(1)}, f32[4,16,64]{2,1,0:T(8,128)S(1)}) custom-call(bf16[4,256]{1,0:T(4,128)(2,1)} %q_hbm.1, s32[4,2,32]{2,1,0:T(2,128)} %list_hbm.1, s32[4,2,8]{2,1,0:T(2,128)} %count_hbm.1, bf16[4,2,1024,128]{3,2,1,0:T(8,128)(2,1)} %k_hbm.1, bf16[4,2,1024,128]{3,2,1,0:T(8,128)(2,1)} %v_hbm.1, ...), custom_call_target="tpu_custom_call" | custom-call | tf_op jit(solution)/shard_map/pallas_call | solution.py:404
  22.5 0.6 %shard_map.86 = (bf16[4,256]{1,0:T(4,128)(2,1)}, bf16[4,256]{1,0:T(4,128)(2,1)}, f32[4,16,64]{2,1,0:T(8,128)}) custom-call(f32[8,128]{1,0:T(8,128)S(1)} %get-tuple-element.6.sum_ref, bf16[4,256]{1,0:T(4,128)(2,1)S(1)} %get-tuple-element.7.attn_in, f32[4,16,64]{2,1,0:T(8,128)S(1)} %get-tuple-element.8.mass_in), custom_call_target="tpu_custom_call" | custom-call | tf_op jit(solution)/shard_map/pallas_call | solution.py:445
